TPU v7x, 32 devices: a whole 2x2x4 slice. The times are simulated.
32 devices in a mesh: rows: 8 (over y, x, core), cols: 4 (over z).
Axes of the slice: x: 2, y: 2, z: 4, core: 2. Of those that a mesh axis runs over, the one named last changes fastest.
Arguments:
- density: bfloat16 [640, 640], P('rows', 'cols'), as said below
- occupancy: int32 [5, 5], replicated, may hold values from 0 to 1, as said below
- square_filter: int32 [5, 5], replicated, may hold values 0 or 1
- cube_filter: int32 [5, 5], replicated, may hold values 0 or 1
Outputs:
- purified: float32 [640, 640], P('rows', 'cols')
Inputs may be any that keep to these rules, and one draw needn't show every extreme that they name: density is symmetric. occupancy is symmetric and every diagonal tile is stored.
All inputs are finite; a program needn't handle non-finite values.
Results may differ from a plain program's by a relative error of at most 0.0095.
Values may be sent and summed in bfloat16 or wider, within the bound.
No kernel may reach another device: no remote copies, remote signals or barrier semaphores. Data moves between devices by JAX's collectives and lax.ppermute only.
A program may use at most 64 MiB of HBM per device.

v0:
```python
import jax
import jax.numpy as jnp
from jax import lax
from jax.sharding import PartitionSpec as P

TILE = 128


def expand(table, row_start, row_count, col_start, col_count):
    count = table.shape[0]
    tile_ids = jnp.arange(count, dtype=jnp.int32)
    row_tiles = (jnp.arange(row_count, dtype=jnp.int32) + row_start) // TILE
    col_tiles = (jnp.arange(col_count, dtype=jnp.int32) + col_start) // TILE
    row_pick = (row_tiles[:, None] == tile_ids[None, :]).astype(jnp.float32)
    col_pick = (tile_ids[:, None] == col_tiles[None, :]).astype(jnp.float32)
    left = jnp.dot(row_pick, table.astype(jnp.float32), precision=lax.Precision.HIGHEST)
    return jnp.dot(left, col_pick, precision=lax.Precision.HIGHEST)


def over_panel(step, init, occupied):
    return step(init, lax.all_gather(occupied, "rows", axis=0, tiled=True), jnp.int32(0))


def on_device(density, occupancy, square_filter, cube_filter):
    row_count, col_count = density.shape
    row_start = lax.axis_index("rows") * row_count
    col_start = lax.axis_index("cols") * col_count
    stored_mask = expand(occupancy, row_start, row_count, col_start, col_count)
    square_mask = expand(square_filter, row_start, row_count, col_start, col_count)
    cube_mask = expand(cube_filter, row_start, row_count, col_start, col_count)
    occupied = jnp.where(stored_mask > 0.5, density, jnp.zeros_like(density))
    empty = jnp.zeros((row_count, col_count), jnp.float32)
    panel = lax.all_gather(occupied, "cols", axis=1, tiled=True)

    def add_square(total, piece, start):
        return jnp.dot(panel, piece, preferred_element_type=jnp.float32)

    square_total = over_panel(add_square, empty, occupied)
    square = jnp.where(square_mask > 0.5, square_total, 0.0).astype(jnp.bfloat16)
    square_rows = lax.all_gather(square, "cols", axis=1, tiled=True)

    def add_cube(total, piece, start):
        return jnp.dot(square_rows, piece, preferred_element_type=jnp.float32)

    cube_total = over_panel(add_cube, empty, occupied)
    cube = jnp.where(cube_mask > 0.5, cube_total, 0.0)
    return 3.0 * square.astype(jnp.float32) - 2.0 * cube


def solution(mesh):
    placed = (P("rows", "cols"), P(), P(), P())
    return jax.shard_map(
        on_device, mesh=mesh, in_specs=placed, out_specs=P("rows", "cols"), check_vma=False
    )
```

profile of v0, /device:TPU:0, one launch (start us, length us, event | category | flops | bytes accessed | tf_op | source)
XLA Modules:
  0.0 42.6 jit_solution(16775872245500241807)
XLA Ops:
  0.0 0.0 copy-start
  0.0 0.9 %fusion.5 = f32[80,5]{1,0:T(8,128)S(1)} fusion(s32[80]{0:T(128)S(1)} %and_select_fusion.1, s32[5,5]{1,0:T(8,128)} %param.5), kind=kOutput, calls=%fused_computation.11 | convolution fusion | flops 24425 | bytes 2020 | tf_op jit(solution)/shard_map/dot_general | solution.py:16
  0.9 0.0 copy-done
  0.9 0.2 fusion.3
  1.1 0.0 copy-start.1
  1.1 0.1 copy.5
  1.2 0.6 %copy-done.1 = s32[5,5]{1,0:T(8,128)S(1)} copy-done((s32[5,5]{1,0:T(8,128)S(1)}, s32[5,5]{1,0:T(8,128)}, u32[]{:S(2)}) %copy-start.1) | copy-done | bytes 124
  1.8 0.2 fusion.6
  2.0 0.0 copy-start.2
  2.0 0.2 convolution_compare_fusion.2
  2.2 0.5 %copy-done.2 = s32[5,5]{1,0:T(8,128)S(1)} copy-done((s32[5,5]{1,0:T(8,128)S(1)}, s32[5,5]{1,0:T(8,128)}, u32[]{:S(2)}) %copy-start.2) | copy-done | bytes 124
  2.7 0.2 fusion.4
  2.9 0.2 convolution_compare_fusion
  3.1 15.2 %all_gather.10 = bf16[80,640]{0,1:T(8,128)(2,1)S(1)} all-gather(bf16[80,160]{0,1:T(8,128)(2,1)S(1)} %copy.5), channel_id=1, replica_groups=mesh['rows'=8,'cols'=4] {'cols'}, dimensions={1}, use_global_device_ids=true | all-gather | bytes 128000 | tf_op jit(solution)/shard_map/all_gather | solution.py:33
  18.3 9.4 %all_gather.11 = bf16[640,160]{1,0:T(8,128)(2,1)S(1)} all-gather(bf16[80,160]{1,0:T(8,128)(2,1)S(1)} %fusion.3), channel_id=1, replica_groups=mesh['rows'=8,'cols'=4] {'rows'}, dimensions={0}, use_global_device_ids=true | all-gather | bytes 230400 | tf_op jit(solution)/shard_map/all_gather | solution.py:21
  27.7 0.2 fusion.2
  27.9 0.1 copy.6
  28.0 13.7 %all_gather.12 = bf16[80,640]{0,1:T(8,128)(2,1)S(1)} all-gather(bf16[80,160]{0,1:T(8,128)(2,1)S(1)} %copy.6), channel_id=1, replica_groups=mesh['rows'=8,'cols'=4] {'cols'}, dimensions={1}, use_global_device_ids=true | all-gather | bytes 128000 | tf_op jit(solution)/shard_map/all_gather | solution.py:40
  41.7 0.9 %fusion.1 = f32[80,160]{1,0:T(8,128)} fusion(pred[80,160]{1,0:T(8,128)(4,1)S(1)} %convolution_compare_fusion, bf16[80,640]{0,1:T(8,128)(2,1)S(1)} %all_gather.12, bf16[640,160]{1,0:T(8,128)(2,1)S(1)} %all_gather.11, bf16[80,160]{1,0:T(8,128)(2,1)S(1)} %fusion.2), kind=kOutput, calls=%fused_computation.3 | convolution fusion | flops 16448000 | bytes 396800 | tf_op jit(solution)/shard_map/dot_general | solution.py:43
  (2 shorter events, 0.0 us)
Async XLA Ops:
  0.0 0.9 %copy-start = (bf16[80,160]{1,0:T(8,128)(2,1)S(1)}, bf16[80,160]{1,0:T(8,128)(2,1)}, u32[]{:S(2)}) copy-start(bf16[80,160]{1,0:T(8,128)(2,1)} %param.4) | copy-start | bytes 76804
  1.1 0.7 %copy-start.1 = (s32[5,5]{1,0:T(8,128)S(1)}, s32[5,5]{1,0:T(8,128)}, u32[]{:S(2)}) copy-start(s32[5,5]{1,0:T(8,128)} %param.6) | copy-start | bytes 304
  2.0 0.7 %copy-start.2 = (s32[5,5]{1,0:T(8,128)S(1)}, s32[5,5]{1,0:T(8,128)}, u32[]{:S(2)}) copy-start(s32[5,5]{1,0:T(8,128)} %param.7) | copy-start | bytes 304
where the time goes:
time: 42.9 us; the launch traced here: 42.6 us
  blocking collectives  38.3 us (89%)
  matrix products  2.92 us (7%)
  local copies, waits for them, and re-layouts  1.3 us (3%)
    all_gather x1, blocking collectives, on_device(): panel = lax.all_gather(occupied, 'cols', axis=1, tiled=True)  15.2 us
    all_gather x1, blocking collectives, on_device(): square_rows = lax.all_gather(square, 'cols', axis=1, tiled=True)  13.7 us
    all_gather x1, blocking collectives, over_panel(): lax.all_gather(occupied, 'rows', axis=0, tiled=True)  9.43 us
    dot_general x3, matrix products, expand(): jnp.dot(row_pick, table.astype(jnp.float32), precision=lax.Precision.HIGH...  1.33 us
    unnamed x6, local copies, waits for them, and re-layouts  1.08 us
    dot_general x1, matrix products, add_cube(): return jnp.dot(square_rows, piece, preferred_element_type=jnp.float32)  0.86 us

commit v1 on v0

--- a/solution.py
+++ b/solution.py
@@ -4,6 +4,19 @@
 from jax.sharding import PartitionSpec as P
 
 TILE = 128
+
+
+def process_screen_on_mesh(mine_x):
+    n = lax.psum(1, "cols")
+    bank = [(hop_no, (hop_no + 1) % n) for hop_no in range(n)]
+
+    def work_stacks_all(b_next):
+        if len(b_next) == n:
+            return b_next
+        return work_stacks_all([lax.ppermute(b_next[0], "cols", perm=bank), *b_next])
+
+    val = jnp.concatenate(work_stacks_all([mine_x]), 1)
+    return jnp.roll(val, (lax.axis_index("cols") + 1) * mine_x.shape[1], 1)
 
 
 def expand(table, row_start, row_count, col_start, col_count):
@@ -30,7 +43,7 @@
     cube_mask = expand(cube_filter, row_start, row_count, col_start, col_count)
     occupied = jnp.where(stored_mask > 0.5, density, jnp.zeros_like(density))
     empty = jnp.zeros((row_count, col_count), jnp.float32)
-    panel = lax.all_gather(occupied, "cols", axis=1, tiled=True)
+    panel = process_screen_on_mesh(occupied)
 
     def add_square(total, piece, start):
         return jnp.dot(panel, piece, preferred_element_type=jnp.float32)

time: 42.9 us -> 39 us (0.909)
  blocking collectives: 38.3 us -> 23.4 us
  waiting for transfers between devices: 0 us -> 8.49 us
  starting transfers between devices: 0 us -> 3.11 us
  local copies, waits for them, and re-layouts: 1.3 us -> 0.79 us
    all_gather x1 -> x0, blocking collectives: 15.2 us -> none  [on_device(): panel = lax.all_gather(occupied, 'cols', axis=1, tiled=True)]
    ppermute x0 -> x3, waiting for transfers between devices: none -> 8.49 us  [work_stacks_all(): lax.ppermute(b_next[0], 'cols', perm=bank)]
    ppermute x0 -> x3, starting transfers between devices: none -> 3.11 us  [work_stacks_all(): lax.ppermute(b_next[0], 'cols', perm=bank)]
    unnamed x6, local copies, waits for them, and re-layouts: 1.08 us -> 0.52 us
  transfers between devices with their start and end apart: 0 -> 3, of which waited for: 0 -> 2; matrix products, arithmetic and copies ran while one was open for 0% -> 2% of each run, Pallas kernels for 0% -> 0%
where the time goes in v1:
time: 39 us; the launch traced here: 38.8 us
  blocking collectives  23.4 us (60%)
  waiting for transfers between devices  8.49 us (22%)
  starting transfers between devices  3.11 us (8%)
  matrix products  2.93 us (8%)
  local copies, waits for them, and re-layouts  0.79 us (2%)
    all_gather x1, blocking collectives, on_device(): square_rows = lax.all_gather(square, 'cols', axis=1, tiled=True)  13.7 us
    all_gather x1, blocking collectives, over_panel(): lax.all_gather(occupied, 'rows', axis=0, tiled=True)  9.65 us
    ppermute x3, waiting for transfers between devices, work_stacks_all(): lax.ppermute(b_next[0], 'cols', perm=bank)  8.49 us
    ppermute x3, starting transfers between devices, work_stacks_all(): lax.ppermute(b_next[0], 'cols', perm=bank)  3.11 us
    dot_general x3, matrix products, expand(): jnp.dot(row_pick, table.astype(jnp.float32), precision=lax.Precision.HIGH...  1.33 us
    dot_general x1, matrix products, add_cube(): return jnp.dot(square_rows, piece, preferred_element_type=jnp.float32)  0.86 us
  transfers between devices with their start and end apart: 3, of which 2 were waited for; matrix products, arithmetic and copies ran while one was open for 2% of the time, Pallas kernels for 0%

profile of v1, /device:TPU:0, one launch (start us, length us, event | category | flops | bytes accessed | tf_op | source)
XLA Modules:
  0.0 38.8 jit_solution(16996158427087671239)
XLA Ops:
  0.0 0.0 copy-start
  0.0 0.9 %fusion.6 = f32[80,5]{1,0:T(8,128)S(1)} fusion(s32[80]{0:T(128)S(1)} %and_select_fusion.1, s32[5,5]{1,0:T(8,128)} %param.5), kind=kOutput, calls=%fused_computation.12 | convolution fusion | flops 24425 | bytes 2020 | tf_op jit(solution)/shard_map/dot_general | solution.py:29
  0.9 0.0 copy-done
  0.9 0.0 copy-start.1
  1.0 0.2 fusion.3
  1.1 3.1 %collective-permute-start = (bf16[80,160]{1,0:T(8,128)(2,1)S(1)}, bf16[80,160]{1,0:T(8,128)(2,1)S(1)}, u32[]{:S(2)}, u32[]{:S(2)}) collective-permute-start(bf16[80,160]{1,0:T(8,128)(2,1)S(1)} %fusion.3), channel_id=1, source_target_pairs={{0,1},{1,2},{2,3},{3,0},{4,5},{5,6},{6,7},{7,4},{8,9},{9,10},{10,1... | collective-permute-start | bytes 76808 | tf_op jit(solution)/shard_map/ppermute | solution.py:16
  4.2 0.0 copy-done.1
  4.2 0.2 fusion.7
  4.5 0.0 copy-start.2
  4.5 0.2 convolution_compare_fusion.2
  4.6 0.5 %copy-done.2 = s32[5,5]{1,0:T(8,128)S(1)} copy-done((s32[5,5]{1,0:T(8,128)S(1)}, s32[5,5]{1,0:T(8,128)}, u32[]{:S(2)}) %copy-start.2) | copy-done | bytes 124
  5.1 0.2 fusion.5
  5.4 2.9 %collective-permute-done = bf16[80,160]{1,0:T(8,128)(2,1)S(1)} collective-permute-done((bf16[80,160]{1,0:T(8,128)(2,1)S(1)}, bf16[80,160]{1,0:T(8,128)(2,1)S(1)}, u32[]{:S(2)}, u32[]{:S(2)}) %collective-permute-start) | collective-permute-done | bytes 25632 | tf_op jit(solution)/shard_map/ppermute | solution.py:16
  8.2 0.0 collective-permute-start.1
  8.2 0.2 convolution_compare_fusion
  8.4 5.6 %collective-permute-done.1 = bf16[80,160]{1,0:T(8,128)(2,1)S(1)} collective-permute-done((bf16[80,160]{1,0:T(8,128)(2,1)S(1)}, bf16[80,160]{1,0:T(8,128)(2,1)S(1)}, u32[]{:S(2)}, u32[]{:S(2)}) %collective-permute-start.1) | collective-permute-done | bytes 25632 | tf_op jit(solution)/shard_map/ppermute | solution.py:16
  14.0 0.0 collective-permute-start.2
  14.0 9.6 %all_gather.7 = bf16[640,160]{1,0:T(8,128)(2,1)S(1)} all-gather(bf16[80,160]{1,0:T(8,128)(2,1)S(1)} %fusion.3), channel_id=1, replica_groups=mesh['rows'=8,'cols'=4] {'rows'}, dimensions={0}, use_global_device_ids=true | all-gather | bytes 230400 | tf_op jit(solution)/shard_map/all_gather | solution.py:34
  23.7 0.0 collective-permute-done.2
  23.7 0.2 concatenate.6
  23.9 0.2 fusion.2
  24.1 0.1 copy.5
  24.2 13.7 %all_gather.8 = bf16[80,640]{0,1:T(8,128)(2,1)S(1)} all-gather(bf16[80,160]{0,1:T(8,128)(2,1)S(1)} %copy.5), channel_id=1, replica_groups=mesh['rows'=8,'cols'=4] {'cols'}, dimensions={1}, use_global_device_ids=true | all-gather | bytes 128000 | tf_op jit(solution)/shard_map/all_gather | solution.py:53
  37.9 0.9 %fusion.1 = f32[80,160]{1,0:T(8,128)} fusion(pred[80,160]{1,0:T(8,128)(4,1)S(1)} %convolution_compare_fusion, bf16[80,640]{0,1:T(8,128)(2,1)S(1)} %all_gather.8, bf16[640,160]{1,0:T(8,128)(2,1)S(1)} %all_gather.7, bf16[80,160]{1,0:T(8,128)(2,1)S(1)} %fusion.2), kind=kOutput, calls=%fused_computation.3 | convolution fusion | flops 16448000 | bytes 396800 | tf_op jit(solution)/shard_map/dot_general | solution.py:56
  (2 shorter events, 0.0 us)
Async XLA Ops:
  0.0 0.9 %copy-start = (bf16[80,160]{1,0:T(8,128)(2,1)S(1)}, bf16[80,160]{1,0:T(8,128)(2,1)}, u32[]{:S(2)}) copy-start(bf16[80,160]{1,0:T(8,128)(2,1)} %param.4) | copy-start | bytes 76804
  0.9 3.3 %copy-start.1 = (s32[5,5]{1,0:T(8,128)S(1)}, s32[5,5]{1,0:T(8,128)}, u32[]{:S(2)}) copy-start(s32[5,5]{1,0:T(8,128)} %param.6) | copy-start | bytes 304
  1.1 7.1 %collective-permute-start = (bf16[80,160]{1,0:T(8,128)(2,1)S(1)}, bf16[80,160]{1,0:T(8,128)(2,1)S(1)}, u32[]{:S(2)}, u32[]{:S(2)}) collective-permute-start(bf16[80,160]{1,0:T(8,128)(2,1)S(1)} %fusion.3), channel_id=1, source_target_pairs={{0,1},{1,2},{2,3},{3,0},{4,5},{5,6},{6,7},{7,4},{8,9},{9,10},{10,1... | collective-permute-start | bytes 76808 | tf_op jit(solution)/shard_map/ppermute | solution.py:16
  4.5 0.7 %copy-start.2 = (s32[5,5]{1,0:T(8,128)S(1)}, s32[5,5]{1,0:T(8,128)}, u32[]{:S(2)}) copy-start(s32[5,5]{1,0:T(8,128)} %param.7) | copy-start | bytes 304
  8.2 5.8 %collective-permute-start.1 = (bf16[80,160]{1,0:T(8,128)(2,1)S(1)}, bf16[80,160]{1,0:T(8,128)(2,1)S(1)}, u32[]{:S(2)}, u32[]{:S(2)}) collective-permute-start(bf16[80,160]{1,0:T(8,128)(2,1)S(1)} %collective-permute-done), channel_id=1, source_target_pairs={{0,1},{1,2},{2,3},{3,0},{4,5},{5,6},{6,7},{7,4},{8,9},{9,10},{10,1... | collective-permute-start | bytes 76808 | tf_op jit(solution)/shard_map/ppermute | solution.py:16
  14.0 9.7 %collective-permute-start.2 = (bf16[80,160]{1,0:T(8,128)(2,1)S(1)}, bf16[80,160]{1,0:T(8,128)(2,1)S(1)}, u32[]{:S(2)}, u32[]{:S(2)}) collective-permute-start(bf16[80,160]{1,0:T(8,128)(2,1)S(1)} %collective-permute-done.1), channel_id=1, source_target_pairs={{0,1},{1,2},{2,3},{3,0},{4,5},{5,6},{6,7},{7,4},{8,9},{9,10},{10,1... | collective-permute-start | bytes 76808 | tf_op jit(solution)/shard_map/ppermute | solution.py:16
